TPU v7x, 32 devices: a whole 2x2x4 slice. The times are simulated.
32 devices in a mesh: row: 8 (over y, x, core), col: 4 (over z).
Axes of the slice: x: 2, y: 2, z: 4, core: 2. Of those that a mesh axis runs over, the one named last changes fastest.
Arguments:
- stiff_bb: bfloat16 [96, 3, 128, 384], P(('row', 'col')), may hold values from -6 to 6
- stiff_bi: bfloat16 [96, 384, 3072], P(('row', 'col')), may hold values from -6 to 6
- constraint_modes: bfloat16 [96, 3072, 384], P(('row', 'col')), may hold values from -0.109375 to 0.109375
- interior_mass: float32 [96, 3072], P(('row', 'col')), may hold values from 0.25 to 4
- fixed_modes: bfloat16 [96, 3072, 256], P(('row', 'col')), may hold values from -6 to 6
- mass_bb: bfloat16 [96, 3, 128, 384], P(('row', 'col')), may hold values from -6 to 6
- boundary_map: int32 [96, 3], P(('row', 'col')), may hold values from 0 to 191, as said below
Outputs:
- interface_stiffness: float32 [192, 4, 128, 128], P('row', None, 'col')
- interface_mass: float32 [192, 4, 128, 128], P('row', None, 'col')
- mass_coupling: float32 [96, 256, 384], P(('row', 'col'))
Inputs may be any that keep to these rules, and one draw needn't show every extreme that they name: `boundary_map`: row s holds blocks b, b + a, b + c with 0 < a < c < 4, all three in the range of one owner (block // 24). Rows come in aligned row groups of 12; no owner serves more than 2 rows of one row group, and in every draw one owner serves exactly 2 rows of every row group.
All inputs are finite; a program needn't handle non-finite values.
Results may differ from a plain program's by a relative error of at most 0.0029.
Values sent between devices are 32-bit elements; how exact they have to be, the bound alone decides.
A program may use at most 192 MiB of HBM per device.

v0:
```python
import functools
import jax
import jax.numpy as jnp
from jax import lax
from jax.experimental import pallas as pl
from jax.experimental.pallas import tpu as pltpu
from jax.sharding import PartitionSpec as P

BAND = 4
BPO = 24
LANE = 128

PAIRS = ((0, 0), (1, 1), (2, 2), (0, 1), (0, 2), (1, 2))
KINDS = 2
CHUNKS = KINDS * len(PAIRS)
MESH = pl.DeviceIdType.MESH
VMEM_LIMIT = 60 * 1024 * 1024


def at_col(z):
    return {"row": lax.axis_index("row"), "col": z}


def at_row(r):
    return {"row": r, "col": lax.axis_index("col")}


def reduce_and_send(
    owners, lanes, slots,
    kbb, kbi, psi, mass, modes, mbb, table,
    got, targets, coupling,
    kbb_v, kbi_v, psi_v, modes_v, mbb_v, weighted, coupled, product,
    reduced, grouped, staging, outgoing, table_v, maps_v, all_v, maps_s, all_s,
    in_sems, z_send, z_recv, r_send, r_recv, r_own,
    zm_send, zm_recv, rm_send, rm_recv, small, out_sems,
):
    count, order, inner = kbi.shape
    width = order // 3
    part = width // lanes
    members = count * lanes
    row = lax.axis_index("row")
    col = lax.axis_index("col")

    def loads(s):
        return (
            pltpu.make_async_copy(kbi.at[s], kbi_v.at[s], in_sems.at[0, s]),
            pltpu.make_async_copy(psi.at[s], psi_v.at[s], in_sems.at[1, s]),
            pltpu.make_async_copy(kbb.at[s], kbb_v.at[s], in_sems.at[2, s]),
        )

    def late_loads(s):
        return (
            pltpu.make_async_copy(mbb.at[s], mbb_v.at[s], in_sems.at[3, s]),
            pltpu.make_async_copy(modes.at[s], modes_v.at[s], in_sems.at[4, s]),
        )

    for copy in loads(0):
        copy.start()

    barrier = pltpu.get_barrier_semaphore()
    for i in range(1, lanes):
        pl.semaphore_signal(barrier, inc=1, device_id=at_col(lax.rem(col + i, lanes)), device_id_type=MESH)

    def greet(i, carry):
        pl.semaphore_signal(barrier, inc=1, device_id=at_row(lax.rem(row + i, owners)), device_id_type=MESH)
        return carry

    lax.fori_loop(1, owners, greet, 0)

    def put(kind, s, total):
        for p, (i, j) in enumerate(PAIRS):
            block = total[i * width : (i + 1) * width, j * width : (j + 1) * width]
            reduced[kind * len(PAIRS) + p, :, s] = block.reshape(lanes, part, width)

    def z_map(i):
        return pltpu.make_async_remote_copy(
            src_ref=table_v, dst_ref=maps_v.at[col],
            send_sem=zm_send.at[i], recv_sem=zm_recv.at[lanes - i],
            device_id=at_col(lax.rem(col + i, lanes)), device_id_type=MESH,
        )

    def z_copy(p, i):
        to = lax.rem(col + i, lanes)
        return pltpu.make_async_remote_copy(
            src_ref=reduced.at[p, to], dst_ref=grouped.at[p, col],
            send_sem=z_send.at[p, i], recv_sem=z_recv.at[p, lanes - i],
            device_id=at_col(to), device_id_type=MESH,
        )

    def z_copy_one(p, s, i):
        to = lax.rem(col + i, lanes)
        return pltpu.make_async_remote_copy(
            src_ref=reduced.at[p, to, s], dst_ref=grouped.at[p, col, s],
            send_sem=z_send.at[p, i], recv_sem=z_recv.at[p, lanes - i],
            device_id=at_col(to), device_id_type=MESH,
        )

    def r_map(i):
        return pltpu.make_async_remote_copy(
            src_ref=maps_v, dst_ref=all_v.at[row],
            send_sem=rm_send.at[i], recv_sem=rm_recv.at[owners - i],
            device_id=at_row(lax.rem(row + i, owners)), device_id_type=MESH,
        )

    half = len(PAIRS)
    place = (lax.broadcasted_iota(jnp.int32, (8, LANE), 0), lax.broadcasted_iota(jnp.int32, (8, LANE), 1))
    tile = jnp.zeros((8, LANE), jnp.int32)
    for s in range(count):
        for k in range(3):
            tile = jnp.where((place[0] == 0) & (place[1] == 3 * s + k), table[s, k], tile)
    table_v[...] = tile
    maps_v[col] = tile

    for s in range(count):
        for copy in loads(s):
            copy.wait()
        if s + 1 < count:
            for copy in loads(s + 1):
                copy.start()
        else:
            for later in range(count):
                for copy in late_loads(later):
                    copy.start()
        product[...] = jnp.dot(kbi_v[s], psi_v[s], preferred_element_type=jnp.float32)
        put(0, s, product[...] + kbb_v[s].astype(jnp.float32).reshape(order, order))
        if s == 0:
            pl.semaphore_wait(barrier, lanes - 1 + owners - 1)
            for i in range(1, lanes):
                z_map(i).start()

        ready = range(s + 1) if s == 0 else range(1, count) if s == count - 1 else ()

        def send_some(p, carry, ready=ready):
            for other in ready:
                for i in range(1, lanes):
                    z_copy_one(p, other, i).start()
            return carry

        if len(ready):
            lax.fori_loop(0, half, send_some, 0)

    def masses(s, carry):
        for copy in late_loads(s):
            copy.wait()
        pick = lax.broadcasted_iota(jnp.int32, (count, inner), 0) == s
        line = jnp.sum(jnp.where(pick, mass[...], 0.0), axis=0, keepdims=True)
        steps = inner // LANE
        lines = [line[:, k * LANE : (k + 1) * LANE] for k in range(steps)]
        filler = jnp.zeros((-steps % LANE, LANE), jnp.float32)
        columns = jnp.concatenate(lines + [filler], axis=0).T
        for k in range(steps):
            span = pl.ds(k * LANE, LANE)
            scale = jnp.broadcast_to(columns[:, k : k + 1], (LANE, order))
            weighted[s, span, :] = (scale * psi_v[s, span, :].astype(jnp.float32)).astype(jnp.bfloat16)
        product[...] = lax.dot_general(psi_v[s], weighted[s], across, preferred_element_type=jnp.float32)
        put(1, s, product[...] + mbb_v[s].astype(jnp.float32).reshape(order, order))
        return carry

    across = (((0,), (0,)), ((), ()))
    lax.fori_loop(0, count, masses, 0)

    def send_chunk(p, carry):
        for i in range(1, lanes):
            z_copy(p, i).start()
        return carry

    lax.fori_loop(half, CHUNKS, send_chunk, 0)
    for i in range(1, lanes):
        z_map(i).wait()
    to_scalar = pltpu.make_async_copy(maps_v, maps_s, small.at[0])
    to_scalar.start()
    lax.fori_loop(1, owners, lambda i, c: (r_map(i).start(), c)[1], 0)
    all_v[row] = maps_v[...]

    def couple(s, carry):
        coupled[s] = lax.dot_general(modes_v[s], weighted[s], across, preferred_element_type=jnp.float32)
        pltpu.make_async_copy(coupled.at[s], coupling.at[s], out_sems.at[s]).start()
        return carry


    def keep(p, carry):
        grouped[p, col] = reduced[p, col]
        return carry

    lax.fori_loop(0, CHUNKS, keep, 0)

    to_scalar.wait()

    belongs = [maps_s[m // count, 0, 3 * (m % count)] // BPO for m in range(members)]
    ranks = []
    for m in range(members):
        rank = jnp.int32(0)
        for e in range(m):
            rank = rank + jnp.where(belongs[e] == belongs[m], 1, 0)
        ranks.append(rank)
    places = [belongs[m] * slots + ranks[m] for m in range(members)]

    chosen = []
    for slot in range(owners * slots):
        member = jnp.int32(0)
        for m in range(1, members):
            member = jnp.where(places[m] == slot, m, member)
        chosen.append(member)

    def forward(p, carry):
        for i in range(1, lanes):
            z_copy(p, i).wait_recv()

        staging[...] = grouped[p].reshape(members, part, width)
        for slot, member in enumerate(chosen):
            outgoing[p, slot // slots, slot % slots] = staging[member]

        def ship(i, inner_carry):
            r_copy(p, i).start()
            return inner_carry

        lax.fori_loop(1, owners, ship, 0)
        own_copy(p).start()
        return carry

    def r_copy(p, i):
        to = lax.rem(row + i, owners)
        return pltpu.make_async_remote_copy(
            src_ref=outgoing.at[p, to], dst_ref=got.at[p, row],
            send_sem=r_send.at[p], recv_sem=r_recv.at[p],
            device_id=at_row(to), device_id_type=MESH,
        )

    def own_copy(p):
        return pltpu.make_async_copy(outgoing.at[p, row], got.at[p, row], r_own.at[p])

    lax.fori_loop(0, count, lambda s, c: couple(s, forward(s, c)), 0)

    lax.fori_loop(1, owners, lambda i, c: (r_map(i).wait(), c)[1], 0)
    all_scalar = pltpu.make_async_copy(all_v.at[:, :, pl.ds(0, 1)], all_s, small.at[1])
    all_scalar.start()
    all_scalar.wait()

    def aim(group, carry):
        picked = [[jnp.int32(-1)] * 3 for _ in range(slots)]
        filled = jnp.int32(0)
        for m in range(members):
            at = [all_s[group, m // count, 0, 3 * (m % count) + k] for k in range(3)]
            mine = at[0] // BPO == row
            for slot in range(slots):
                hit = mine & (filled == slot)
                picked[slot] = [jnp.where(hit, at[k], picked[slot][k]) for k in range(3)]
            filled = filled + jnp.where(mine, 1, 0)
        for slot in range(slots):
            at = picked[slot]
            for p, (i, j) in enumerate(PAIRS):
                local = (at[i] - row * BPO) * BAND + at[j] - at[i]
                targets[p, group * slots + slot] = jnp.where(at[0] >= 0, local, BPO * BAND)
        return carry

    lax.fori_loop(0, owners, aim, 0)
    lax.fori_loop(count, CHUNKS, forward, 0)

    def settle(p, carry):
        for i in range(1, lanes):
            z_copy(p, i).wait_send()
        rest = got.at[p, pl.ds(0, owners - 1)]
        pltpu.make_async_copy(rest, rest, r_send.at[p]).wait()
        pltpu.make_async_copy(rest, rest, r_recv.at[p]).wait()
        own_copy(p).wait()
        return carry

    lax.fori_loop(0, CHUNKS, settle, 0)
    for s in range(count):
        pltpu.make_async_copy(coupled.at[s], coupling.at[s], out_sems.at[s]).wait()


def assemble(
    owners, slots, targets, got, coupled, k_out, m_out, coupling,
    buffer, band, passing, in_sems, out_sems, pass_sems,
):
    limit = BPO * BAND

    def load(p):
        return pltpu.make_async_copy(got.at[p], buffer.at[p], in_sems.at[p])

    for p in range(CHUNKS):
        load(p).start()
    inward = pltpu.make_async_copy(coupled, passing, pass_sems.at[0])
    inward.start()
    band[...] = jnp.zeros_like(band)
    writes = []
    for kind, out in enumerate((k_out, m_out)):
        for p in range(len(PAIRS)):
            chunk = kind * len(PAIRS) + p
            load(chunk).wait()
            for place in range(owners * slots):
                at = targets[p, place]
                band[kind, at] += buffer[chunk, place // slots, place % slots]
        writes.append(pltpu.make_async_copy(band.at[kind, pl.ds(0, limit)], out, out_sems.at[kind]))
        writes[-1].start()
        if kind == 0:
            inward.wait()
            writes.append(pltpu.make_async_copy(passing, coupling, pass_sems.at[1]))
            writes[-1].start()
    for write in writes:
        write.wait()


def per_device(
    stiff_bb, stiff_bi, constraint_modes, interior_mass, fixed_modes, mass_bb, boundary_map
):
    owners = lax.axis_size("row")
    lanes = lax.axis_size("col")
    count, order, inner = stiff_bi.shape
    modes = fixed_modes.shape[2]
    width = order // 3
    part = width // lanes
    slots = (count * lanes + owners - 1) // owners
    f32, bf16 = jnp.float32, jnp.bfloat16
    hbm = pl.BlockSpec(memory_space=pl.ANY)
    vmem = pl.BlockSpec(memory_space=pltpu.VMEM)
    smem = pl.BlockSpec(memory_space=pltpu.SMEM)
    dma = pltpu.SemaphoreType.DMA
    got, targets, coupled = pl.pallas_call(
        functools.partial(reduce_and_send, owners, lanes, slots),
        out_shape=(
            jax.ShapeDtypeStruct((CHUNKS, owners, slots, part, width), f32),
            jax.ShapeDtypeStruct((len(PAIRS), owners * slots), jnp.int32),
            jax.ShapeDtypeStruct((count, modes, order), f32),
        ),
        in_specs=[hbm, hbm, hbm, vmem, hbm, hbm, smem],
        out_specs=(hbm, smem, hbm),
        scratch_shapes=[
            pltpu.VMEM((count, 3, width, order), bf16),
            pltpu.VMEM((count, order, inner), bf16),
            pltpu.VMEM((count, inner, order), bf16),
            pltpu.VMEM((count, inner, modes), bf16),
            pltpu.VMEM((count, 3, width, order), bf16),
            pltpu.VMEM((count, inner, order), bf16),
            pltpu.VMEM((count, modes, order), f32),
            pltpu.VMEM((order, order), f32),
            pltpu.VMEM((CHUNKS, lanes, count, part, width), f32),
            pltpu.VMEM((CHUNKS, lanes, count, part, width), f32),
            pltpu.VMEM((lanes * count, part, width), f32),
            pltpu.VMEM((CHUNKS, owners, slots, part, width), f32),
            pltpu.VMEM((8, LANE), jnp.int32),
            pltpu.VMEM((lanes, 8, LANE), jnp.int32),
            pltpu.VMEM((owners, lanes, 8, LANE), jnp.int32),
            pltpu.SMEM((lanes, 8, LANE), jnp.int32),
            pltpu.SMEM((owners, lanes, 1, LANE), jnp.int32),
            dma((5, count)),
            dma((CHUNKS, lanes)),
            dma((CHUNKS, lanes)),
            dma((CHUNKS,)),
            dma((CHUNKS,)),
            dma((CHUNKS,)),
            dma((lanes,)),
            dma((lanes,)),
            dma((owners,)),
            dma((owners,)),
            dma((2,)),
            dma((count,)),
        ],
        compiler_params=pltpu.CompilerParams(
            collective_id=0, has_side_effects=True, vmem_limit_bytes=VMEM_LIMIT
        ),
        name="reduce_and_send",
    )(stiff_bb, stiff_bi, constraint_modes, interior_mass, fixed_modes, mass_bb, boundary_map)
    block = jax.ShapeDtypeStruct((BPO * BAND, part, width), f32)
    k_out, m_out, coupling = pl.pallas_call(
        functools.partial(assemble, owners, slots),
        out_shape=(block, block, jax.ShapeDtypeStruct(coupled.shape, f32)),
        in_specs=[smem, hbm, hbm],
        out_specs=(hbm, hbm, hbm),
        scratch_shapes=[
            pltpu.VMEM(got.shape, f32),
            pltpu.VMEM((KINDS, BPO * BAND + 1, part, width), f32),
            pltpu.VMEM(coupled.shape, f32),
            dma((CHUNKS,)),
            dma((KINDS,)),
            dma((2,)),
        ],
        compiler_params=pltpu.CompilerParams(vmem_limit_bytes=VMEM_LIMIT),
        name="assemble",
    )(targets, got, coupled)
    shape = (BPO, BAND, part, width)
    return k_out.reshape(shape), m_out.reshape(shape), coupling


def solution(mesh):
    placed = (
        P(("row", "col"), None, None, None),
        P(("row", "col"), None, None),
        P(("row", "col"), None, None),
        P(("row", "col"), None),
        P(("row", "col"), None, None),
        P(("row", "col"), None, None, None),
        P(("row", "col"), None),
    )
    return jax.shard_map(
        per_device,
        mesh=mesh,
        in_specs=placed,
        out_specs=(
            P("row", None, "col", None),
            P("row", None, "col", None),
            P(("row", "col"), None, None),
        ),
        check_vma=False,
    )
```

profile of v0, /device:TPU:0, one launch (start us, length us, event | category | flops | bytes accessed | tf_op | source)
XLA Modules:
  0.0 75.7 jit_solution(17775717935611602026)
XLA Ops:
  0.6 70.5 %reduce_and_send.1 = (f32[12,8,2,32,128]{4,3,2,1,0:T(8,128)}, s32[6,16]{1,0:T(8,128)}, f32[3,256,384]{2,1,0:T(8,128)}) custom-call(bf16[3,3,128,384]{3,2,1,0:T(8,128)(2,1)} %kbb.1, bf16[3,384,3072]{2,1,0:T(8,128)(2,1)} %kbi.1, bf16[3,3072,384]{2,1,0:T(8,128)(2,1)} %psi.1, f32[3,3072]{1,0:T(4,128)} %mass.1, bf16[3,3072,256]{2,1,0:T(8,128)(2,1)} %modes.1, ...), custom_call_target="tpu_custom_call" | custom-call | tf_op jit(solution)/shard_map/reduce_and_send/pallas_call | solution.py:320
  71.1 4.6 %assemble.1 = (f32[96,32,128]{2,1,0:T(8,128)}, f32[96,32,128]{2,1,0:T(8,128)}, f32[3,256,384]{2,1,0:T(8,128)}) custom-call(s32[6,16]{1,0:T(8,128)} %get-tuple-element.9.targets, f32[12,8,2,32,128]{4,3,2,1,0:T(8,128)} %get-tuple-element.10.got, f32[3,256,384]{2,1,0:T(8,128)} %get-tuple-element.11.coupled), custom_call_target="tpu_custom_call" | custom-call | tf_op jit(solution)/shard_map/assemble/pallas_call | solution.py:366
where the time goes:
time: 76 us; the launch traced here: 75.7 us
  Pallas kernels  75.1 us (99%)
    pallas_call x1, Pallas kernels, per_device(): pl.pallas_call(functools.partial(reduce_and_send, owners, lanes, slots),...  70.5 us
    pallas_call x1, Pallas kernels, per_device(): pl.pallas_call(functools.partial(assemble, owners, slots), out_shape=(blo...  4.62 us

commit v1 on v0

--- a/solution.py
+++ b/solution.py
@@ -10,9 +10,11 @@
 BPO = 24
 LANE = 128
 
-PAIRS = ((0, 0), (1, 1), (2, 2), (0, 1), (0, 2), (1, 2))
+PAIRS = ((0, 0), (0, 1), (1, 1), (1, 2), (2, 2), (0, 2))
 KINDS = 2
 CHUNKS = KINDS * len(PAIRS)
+AHEAD = 2
+PIECES = 4
 MESH = pl.DeviceIdType.MESH
 VMEM_LIMIT = 60 * 1024 * 1024
 
@@ -29,10 +31,10 @@
     owners, lanes, slots,
     kbb, kbi, psi, mass, modes, mbb, table,
     got, targets, coupling,
-    kbb_v, kbi_v, psi_v, modes_v, mbb_v, weighted, coupled, product,
+    kbb_v, kbi_v, psi_v, modes_v, mbb_v, weighted, coupled,
     reduced, grouped, staging, outgoing, table_v, maps_v, all_v, maps_s, all_s,
     in_sems, z_send, z_recv, r_send, r_recv, r_own,
-    zm_send, zm_recv, rm_send, rm_recv, small, out_sems,
+    zm_send, zm_recv, rm_send, rm_recv, small, out_sems, block_sems, piece_sems,
 ):
     count, order, inner = kbi.shape
     width = order // 3
@@ -41,11 +43,22 @@
     row = lax.axis_index("row")
     col = lax.axis_index("col")
 
+    def block_load(i):
+        span = pl.ds(i * width, width)
+        return pltpu.make_async_copy(kbi.at[0, span], kbi_v.at[0, span], block_sems.at[i])
+
+    def piece_load(k):
+        span = pl.ds(k * (inner // PIECES), inner // PIECES)
+        return pltpu.make_async_copy(psi.at[0, span], psi_v.at[0, span], piece_sems.at[k])
+
+    def kbb_load(s):
+        return pltpu.make_async_copy(kbb.at[s], kbb_v.at[s], in_sems.at[2, s])
+
     def loads(s):
         return (
             pltpu.make_async_copy(kbi.at[s], kbi_v.at[s], in_sems.at[0, s]),
             pltpu.make_async_copy(psi.at[s], psi_v.at[s], in_sems.at[1, s]),
-            pltpu.make_async_copy(kbb.at[s], kbb_v.at[s], in_sems.at[2, s]),
+            kbb_load(s),
         )
 
     def late_loads(s):
@@ -54,8 +67,12 @@
             pltpu.make_async_copy(modes.at[s], modes_v.at[s], in_sems.at[4, s]),
         )
 
-    for copy in loads(0):
-        copy.start()
+    block_load(0).start()
+    for k in range(PIECES):
+        piece_load(k).start()
+    kbb_load(0).start()
+    for i in range(1, 3):
+        block_load(i).start()
 
     barrier = pltpu.get_barrier_semaphore()
     for i in range(1, lanes):
@@ -67,10 +84,17 @@
 
     lax.fori_loop(1, owners, greet, 0)
 
-    def put(kind, s, total):
-        for p, (i, j) in enumerate(PAIRS):
-            block = total[i * width : (i + 1) * width, j * width : (j + 1) * width]
-            reduced[kind * len(PAIRS) + p, :, s] = block.reshape(lanes, part, width)
+    def put(kind, s, i, strip):
+        for j in range(i, 3):
+            block = strip[:, (j - i) * width : (j - i + 1) * width]
+            reduced[kind * len(PAIRS) + PAIRS.index((i, j)), :, s] = block.reshape(lanes, part, width)
+
+    def stiff(s, i):
+        strip = jnp.dot(
+            kbi_v[s, i * width : (i + 1) * width, :], psi_v[s, :, i * width :],
+            preferred_element_type=jnp.float32,
+        )
+        put(0, s, i, strip + kbb_v[s, i, :, i * width :].astype(jnp.float32))
 
     def z_map(i):
         return pltpu.make_async_remote_copy(
@@ -87,10 +111,10 @@
             device_id=at_col(to), device_id_type=MESH,
         )
 
-    def z_copy_one(p, s, i):
+    def z_copy_part(p, first, size, i):
         to = lax.rem(col + i, lanes)
         return pltpu.make_async_remote_copy(
-            src_ref=reduced.at[p, to, s], dst_ref=grouped.at[p, col, s],
+            src_ref=reduced.at[p, to, pl.ds(first, size)], dst_ref=grouped.at[p, col, pl.ds(first, size)],
             send_sem=z_send.at[p, i], recv_sem=z_recv.at[p, lanes - i],
             device_id=at_col(to), device_id_type=MESH,
         )
@@ -111,33 +135,47 @@
     table_v[...] = tile
     maps_v[col] = tile
 
+    for k in range(PIECES):
+        piece_load(k).wait()
+    kbb_load(0).wait()
+    for i in range(3):
+        block_load(i).wait()
+        if i == 0:
+            for later in range(1, count):
+                for copy in loads(later):
+                    copy.start()
+        stiff(0, i)
+        if i == 0:
+            pl.semaphore_wait(barrier, lanes - 1 + owners - 1)
+            for k in range(1, lanes):
+                z_map(k).start()
+        for j in range(i, 3):
+            for k in range(1, lanes):
+                z_copy_part(PAIRS.index((i, j)), 0, 1, k).start()
+
     for s in range(count):
+        for copy in late_loads(s):
+            copy.start()
+
+    def stiffs(s, carry):
         for copy in loads(s):
             copy.wait()
-        if s + 1 < count:
-            for copy in loads(s + 1):
-                copy.start()
-        else:
-            for later in range(count):
-                for copy in late_loads(later):
-                    copy.start()
-        product[...] = jnp.dot(kbi_v[s], psi_v[s], preferred_element_type=jnp.float32)
-        put(0, s, product[...] + kbb_v[s].astype(jnp.float32).reshape(order, order))
-        if s == 0:
-            pl.semaphore_wait(barrier, lanes - 1 + owners - 1)
-            for i in range(1, lanes):
-                z_map(i).start()
-
-        ready = range(s + 1) if s == 0 else range(1, count) if s == count - 1 else ()
-
-        def send_some(p, carry, ready=ready):
-            for other in ready:
-                for i in range(1, lanes):
-                    z_copy_one(p, other, i).start()
-            return carry
-
-        if len(ready):
-            lax.fori_loop(0, half, send_some, 0)
+        for i in range(3):
+            stiff(s, i)
+        return carry
+
+    lax.fori_loop(1, count, stiffs, 0)
+
+    def send_rest(p):
+        for i in range(1, lanes):
+            z_copy_part(p, 1, count - 1, i).start()
+
+    def send_chunk(p):
+        for i in range(1, lanes):
+            z_copy(p, i).start()
+
+    for p in range(AHEAD):
+        send_rest(p)
 
     def masses(s, carry):
         for copy in late_loads(s):
@@ -152,19 +190,17 @@
             span = pl.ds(k * LANE, LANE)
             scale = jnp.broadcast_to(columns[:, k : k + 1], (LANE, order))
             weighted[s, span, :] = (scale * psi_v[s, span, :].astype(jnp.float32)).astype(jnp.bfloat16)
-        product[...] = lax.dot_general(psi_v[s], weighted[s], across, preferred_element_type=jnp.float32)
-        put(1, s, product[...] + mbb_v[s].astype(jnp.float32).reshape(order, order))
+        for i in range(3):
+            strip = lax.dot_general(
+                psi_v[s, :, i * width : (i + 1) * width], weighted[s, :, i * width :], across,
+                preferred_element_type=jnp.float32,
+            )
+            put(1, s, i, strip + mbb_v[s, i, :, i * width :].astype(jnp.float32))
         return carry
 
     across = (((0,), (0,)), ((), ()))
     lax.fori_loop(0, count, masses, 0)
 
-    def send_chunk(p, carry):
-        for i in range(1, lanes):
-            z_copy(p, i).start()
-        return carry
-
-    lax.fori_loop(half, CHUNKS, send_chunk, 0)
     for i in range(1, lanes):
         z_map(i).wait()
     to_scalar = pltpu.make_async_copy(maps_v, maps_s, small.at[0])
@@ -183,6 +219,7 @@
         return carry
 
     lax.fori_loop(0, CHUNKS, keep, 0)
+    lax.fori_loop(0, count, couple, 0)
 
     to_scalar.wait()
 
@@ -202,9 +239,11 @@
             member = jnp.where(places[m] == slot, m, member)
         chosen.append(member)
 
-    def forward(p, carry):
+    def forward(send, p, carry):
         for i in range(1, lanes):
             z_copy(p, i).wait_recv()
+        if send is not None:
+            send(p + AHEAD)
 
         staging[...] = grouped[p].reshape(members, part, width)
         for slot, member in enumerate(chosen):
@@ -228,8 +267,6 @@
 
     def own_copy(p):
         return pltpu.make_async_copy(outgoing.at[p, row], got.at[p, row], r_own.at[p])
-
-    lax.fori_loop(0, count, lambda s, c: couple(s, forward(s, c)), 0)
 
     lax.fori_loop(1, owners, lambda i, c: (r_map(i).wait(), c)[1], 0)
     all_scalar = pltpu.make_async_copy(all_v.at[:, :, pl.ds(0, 1)], all_s, small.at[1])
@@ -254,7 +291,9 @@
         return carry
 
     lax.fori_loop(0, owners, aim, 0)
-    lax.fori_loop(count, CHUNKS, forward, 0)
+    lax.fori_loop(0, half - AHEAD, functools.partial(forward, send_rest), 0)
+    lax.fori_loop(half - AHEAD, CHUNKS - AHEAD, functools.partial(forward, send_chunk), 0)
+    lax.fori_loop(CHUNKS - AHEAD, CHUNKS, functools.partial(forward, None), 0)
 
     def settle(p, carry):
         for i in range(1, lanes):
@@ -334,7 +373,6 @@
             pltpu.VMEM((count, 3, width, order), bf16),
             pltpu.VMEM((count, inner, order), bf16),
             pltpu.VMEM((count, modes, order), f32),
-            pltpu.VMEM((order, order), f32),
             pltpu.VMEM((CHUNKS, lanes, count, part, width), f32),
             pltpu.VMEM((CHUNKS, lanes, count, part, width), f32),
             pltpu.VMEM((lanes * count, part, width), f32),
@@ -356,6 +394,8 @@
             dma((owners,)),
             dma((2,)),
             dma((count,)),
+            dma((3,)),
+            dma((PIECES,)),
         ],
         compiler_params=pltpu.CompilerParams(
             collective_id=0, has_side_effects=True, vmem_limit_bytes=VMEM_LIMIT

time: 76 us -> 71.2 us (0.937)
  Pallas kernels: 75.1 us -> 70.3 us
    pallas_call x1, Pallas kernels: 70.5 us -> 65.7 us  [per_device(): pl.pallas_call(functools.partial(reduce_and_send, owners, lanes, slots),...]
where the time goes in v1:
time: 71.2 us; the launch traced here: 70.9 us
  Pallas kernels  70.3 us (99%)
    pallas_call x1, Pallas kernels, per_device(): pl.pallas_call(functools.partial(reduce_and_send, owners, lanes, slots),...  65.7 us
    pallas_call x1, Pallas kernels, per_device(): pl.pallas_call(functools.partial(assemble, owners, slots), out_shape=(blo...  4.62 us

profile of v1, /device:TPU:0, one launch (start us, length us, event | category | flops | bytes accessed | tf_op | source)
XLA Modules:
  0.0 70.9 jit_solution(11352050920995202557)
XLA Ops:
  0.6 65.7 %reduce_and_send.1 = (f32[12,8,2,32,128]{4,3,2,1,0:T(8,128)}, s32[6,16]{1,0:T(8,128)}, f32[3,256,384]{2,1,0:T(8,128)}) custom-call(bf16[3,3,128,384]{3,2,1,0:T(8,128)(2,1)} %kbb.1, bf16[3,384,3072]{2,1,0:T(8,128)(2,1)} %kbi.1, bf16[3,3072,384]{2,1,0:T(8,128)(2,1)} %psi.1, f32[3,3072]{1,0:T(4,128)} %mass.1, bf16[3,3072,256]{2,1,0:T(8,128)(2,1)} %modes.1, ...), custom_call_target="tpu_custom_call" | custom-call | tf_op jit(solution)/shard_map/reduce_and_send/pallas_call | solution.py:359
  66.3 4.6 %assemble.1 = (f32[96,32,128]{2,1,0:T(8,128)}, f32[96,32,128]{2,1,0:T(8,128)}, f32[3,256,384]{2,1,0:T(8,128)}) custom-call(s32[6,16]{1,0:T(8,128)} %get-tuple-element.9.targets, f32[12,8,2,32,128]{4,3,2,1,0:T(8,128)} %get-tuple-element.10.got, f32[3,256,384]{2,1,0:T(8,128)} %get-tuple-element.11.coupled), custom_call_target="tpu_custom_call" | custom-call | tf_op jit(solution)/shard_map/assemble/pallas_call | solution.py:406

commit v2 on v1

v2 whole, which is shorter than its diff:
```python
import functools
import jax
import jax.numpy as jnp
from jax import lax
from jax.experimental import pallas as pl
from jax.experimental.pallas import tpu as pltpu
from jax.sharding import PartitionSpec as P

BAND = 4
BPO = 24
LANE = 128

PAIRS = ((0, 0), (0, 1), (1, 1), (1, 2), (2, 2), (0, 2))
KINDS = 2
SPLIT = 1
CHUNKS = KINDS * len(PAIRS) * SPLIT
AHEAD = 2
LEAD = 4
PIECES = 4
MESH = pl.DeviceIdType.MESH
VMEM_LIMIT = 46 * 1024 * 1024
BAND_LIMIT = 12 * 1024 * 1024


def at_col(z):
    return {"row": lax.axis_index("row"), "col": z}


def at_row(r):
    return {"row": r, "col": lax.axis_index("col")}


def reduce_and_send(
    owners, lanes, slots,
    kbb, kbi, psi, mass, modes, mbb, table,
    got, targets, coupled,
    kbb_v, kbi_v, psi_v, modes_v, mbb_v, mass_v, weighted,
    reduced, grouped, staging, outgoing, table_v, maps_v, all_v, table_s, maps_s, all_s,
    load_sems, z_send, z_recv, r_sems, map_sems, small, block_sems,
):
    count, order, inner = kbi.shape
    width = order // 3
    part = width // lanes
    rows = part // SPLIT
    members = count * lanes
    row = lax.axis_index("row")
    col = lax.axis_index("col")

    def block_load(i):
        span = pl.ds(i * width, width)
        return pltpu.make_async_copy(kbi.at[0, span], kbi_v.at[0, span], block_sems.at[i])

    def piece_load(k):
        span = pl.ds(k * (inner // PIECES), inner // PIECES)
        return pltpu.make_async_copy(psi.at[0, span], psi_v.at[0, span], load_sems.at[1, 0])

    def loads(s):
        return (
            pltpu.make_async_copy(kbi.at[s], kbi_v.at[s], load_sems.at[0, s]),
            pltpu.make_async_copy(psi.at[s], psi_v.at[s], load_sems.at[1, s]),
        )

    first_kbb = pltpu.make_async_copy(kbb.at[0], kbb_v.at[0], small.at[0])
    others = pl.ds(1, count - 1)
    other_kbb = pltpu.make_async_copy(kbb.at[others], kbb_v.at[others], small.at[1])
    late_loads = (
        pltpu.make_async_copy(mass, mass_v, small.at[2]),
        pltpu.make_async_copy(mbb, mbb_v, small.at[3]),
        pltpu.make_async_copy(modes, modes_v, small.at[4]),
    )

    table_load = pltpu.make_async_copy(table, table_s, small.at[5])
    table_load.start()
    block_load(0).start()
    for k in range(PIECES):
        piece_load(k).start()
    first_kbb.start()
    for i in range(1, 3):
        block_load(i).start()

    barrier = pltpu.get_barrier_semaphore()
    for i in range(1, lanes):
        pl.semaphore_signal(barrier, inc=1, device_id=at_col(lax.rem(col + i, lanes)), device_id_type=MESH)

    def greet(i, carry):
        pl.semaphore_signal(barrier, inc=1, device_id=at_row(lax.rem(row + i, owners)), device_id_type=MESH)
        return carry

    lax.fori_loop(1, owners, greet, 0)

    def put(kind, s, i, strip):
        for j in range(i, 3):
            block = strip[:, (j - i) * width : (j - i + 1) * width].reshape(lanes, SPLIT, rows, width)
            for h in range(SPLIT):
                reduced[(kind * len(PAIRS) + PAIRS.index((i, j))) * SPLIT + h, :, s] = block[:, h]

    def stiff(s, i):
        strip = jnp.dot(
            kbi_v[s, i * width : (i + 1) * width, :], psi_v[s, :, i * width :],
            preferred_element_type=jnp.float32,
        )
        put(0, s, i, strip + kbb_v[s, i, :, i * width :].astype(jnp.float32))

    def drain(ref, sem):
        pltpu.make_async_copy(ref, ref, sem).wait()

    def z_map(i):
        return pltpu.make_async_remote_copy(
            src_ref=table_v, dst_ref=maps_v.at[col],
            send_sem=map_sems.at[0], recv_sem=map_sems.at[1],
            device_id=at_col(lax.rem(col + i, lanes)), device_id_type=MESH,
        )

    def z_copy(p, i):
        to = lax.rem(col + i, lanes)
        return pltpu.make_async_remote_copy(
            src_ref=reduced.at[p, to], dst_ref=grouped.at[p, col],
            send_sem=z_send, recv_sem=z_recv.at[p],
            device_id=at_col(to), device_id_type=MESH,
        )

    def z_copy_part(p, first, size, i):
        to = lax.rem(col + i, lanes)
        return pltpu.make_async_remote_copy(
            src_ref=reduced.at[p, to, pl.ds(first, size)], dst_ref=grouped.at[p, col, pl.ds(first, size)],
            send_sem=z_send, recv_sem=z_recv.at[p],
            device_id=at_col(to), device_id_type=MESH,
        )

    def r_map(i):
        return pltpu.make_async_remote_copy(
            src_ref=maps_v, dst_ref=all_v.at[row],
            send_sem=map_sems.at[2], recv_sem=map_sems.at[3],
            device_id=at_row(lax.rem(row + i, owners)), device_id_type=MESH,
        )

    half = CHUNKS // KINDS
    table_load.wait()
    place = (lax.broadcasted_iota(jnp.int32, (8, LANE), 0), lax.broadcasted_iota(jnp.int32, (8, LANE), 1))
    tile = jnp.zeros((8, LANE), jnp.int32)
    for s in range(count):
        for k in range(3):
            tile = jnp.where((place[0] == 0) & (place[1] == 3 * s + k), table_s[s, k], tile)
    table_v[...] = tile
    maps_v[col] = tile

    loads(0)[1].wait()
    first_kbb.wait()
    for i in range(3):
        block_load(i).wait()
        if i == 0:
            for later in range(1, count):
                for copy in loads(later):
                    copy.start()
            other_kbb.start()
            for copy in late_loads:
                copy.start()
        stiff(0, i)
        if i == 0:
            pl.semaphore_wait(barrier, lanes - 1 + owners - 1)
            for k in range(1, lanes):
                z_map(k).start()
        for j in range(i, 3):
            for h in range(SPLIT):
                for k in range(1, lanes):
                    z_copy_part(PAIRS.index((i, j)) * SPLIT + h, 0, 1, k).start()

    other_kbb.wait()

    def stiffs(s, carry):
        for copy in loads(s):
            copy.wait()
        for i in range(3):
            stiff(s, i)
        return carry

    lax.fori_loop(1, count, stiffs, 0)

    def send_rest(p):
        for i in range(1, lanes):
            z_copy_part(p, 1, count - 1, i).start()

    def send_chunk(p):
        for i in range(1, lanes):
            z_copy(p, i).start()

    for p in range(LEAD):
        send_rest(p)

    def masses(s, carry):
        pick = lax.broadcasted_iota(jnp.int32, (count, inner), 0) == s
        line = jnp.sum(jnp.where(pick, mass_v[...], 0.0), axis=0, keepdims=True)
        steps = inner // LANE
        lines = [line[:, k * LANE : (k + 1) * LANE] for k in range(steps)]
        filler = jnp.zeros((-steps % LANE, LANE), jnp.float32)
        columns = jnp.concatenate(lines + [filler], axis=0).T
        for k in range(steps):
            span = pl.ds(k * LANE, LANE)
            scale = jnp.broadcast_to(columns[:, k : k + 1], (LANE, order))
            weighted[s, span, :] = (scale * psi_v[s, span, :].astype(jnp.float32)).astype(jnp.bfloat16)
        for i in range(3):
            strip = lax.dot_general(
                psi_v[s, :, i * width : (i + 1) * width], weighted[s, :, i * width :], across,
                preferred_element_type=jnp.float32,
            )
            put(1, s, i, strip + mbb_v[s, i, :, i * width :].astype(jnp.float32))
        return carry

    across = (((0,), (0,)), ((), ()))
    for copy in late_loads:
        copy.wait()
    lax.fori_loop(0, count, masses, 0)

    for k in range(2):
        drain(maps_v.at[pl.ds(0, lanes - 1)], map_sems.at[k])
    to_scalar = pltpu.make_async_copy(maps_v, maps_s, small.at[6])
    to_scalar.start()
    lax.fori_loop(1, owners, lambda i, c: (r_map(i).start(), c)[1], 0)
    all_v[row] = maps_v[...]

    def couple(s, carry):
        coupled[s] = lax.dot_general(modes_v[s], weighted[s], across, preferred_element_type=jnp.float32)
        return carry

    def keep(p, carry):
        grouped[p, col] = reduced[p, col]
        return carry

    lax.fori_loop(0, CHUNKS, keep, 0)
    lax.fori_loop(0, count, couple, 0)

    to_scalar.wait()

    belongs = [maps_s[m // count, 0, 3 * (m % count)] // BPO for m in range(members)]
    ranks = []
    for m in range(members):
        rank = jnp.int32(0)
        for e in range(m):
            rank = rank + jnp.where(belongs[e] == belongs[m], 1, 0)
        ranks.append(rank)
    places = [belongs[m] * slots + ranks[m] for m in range(members)]

    chosen = []
    for slot in range(owners * slots):
        member = jnp.int32(0)
        for m in range(1, members):
            member = jnp.where(places[m] == slot, m, member)
        chosen.append(member)

    def forward(send, p, carry):
        drain(grouped.at[p, pl.ds(0, lanes - 1)], z_recv.at[p])
        if send is not None:
            send(p)

        staging[...] = grouped[p].reshape(members, rows, width)
        for slot, member in enumerate(chosen):
            outgoing[p, slot // slots, slot % slots] = staging[member]

        def ship(i, inner_carry):
            r_copy(p, i).start()
            return inner_carry

        lax.fori_loop(1, owners, ship, 0)
        got[p, row] = outgoing[p, row]
        return carry

    def r_copy(p, i):
        to = lax.rem(row + i, owners)
        return pltpu.make_async_remote_copy(
            src_ref=outgoing.at[p, to], dst_ref=got.at[p, row],
            send_sem=r_sems.at[0], recv_sem=r_sems.at[1],
            device_id=at_row(to), device_id_type=MESH,
        )

    for k in range(2, 4):
        drain(all_v.at[pl.ds(0, owners - 1)], map_sems.at[k])
    all_scalar = pltpu.make_async_copy(all_v.at[:, :, pl.ds(0, 1)], all_s, small.at[7])
    all_scalar.start()
    all_scalar.wait()

    def aim(group, carry):
        picked = [[jnp.int32(-1)] * 3 for _ in range(slots)]
        filled = jnp.int32(0)
        for m in range(members):
            at = [all_s[group, m // count, 0, 3 * (m % count) + k] for k in range(3)]
            mine = at[0] // BPO == row
            for slot in range(slots):
                hit = mine & (filled == slot)
                picked[slot] = [jnp.where(hit, at[k], picked[slot][k]) for k in range(3)]
            filled = filled + jnp.where(mine, 1, 0)
        for slot in range(slots):
            at = picked[slot]
            for p, (i, j) in enumerate(PAIRS):
                local = (at[i] - row * BPO) * BAND + at[j] - at[i]
                targets[p, group * slots + slot] = jnp.where(at[0] >= 0, local, BPO * BAND)
        return carry

    lax.fori_loop(0, owners, aim, 0)
    def follow(first, last, send):
        lax.fori_loop(first, last, functools.partial(forward, send), 0)

    follow(0, half - LEAD, lambda p: send_rest(p + LEAD))
    follow(half - LEAD, half - AHEAD, None)
    follow(half - AHEAD, CHUNKS - AHEAD, lambda p: send_chunk(p + AHEAD))
    follow(CHUNKS - AHEAD, CHUNKS, None)

    drain(grouped.at[:, pl.ds(0, lanes - 1)], z_send)
    for k in range(2):
        drain(got.at[:, pl.ds(0, owners - 1)], r_sems.at[k])


def assemble(owners, slots, targets, got, coupled, k_out, m_out, coupling, band, out_sems):
    limit = BPO * BAND
    writes = [pltpu.make_async_copy(coupled, coupling, out_sems.at[KINDS])]
    writes[0].start()
    for kind, out in enumerate((k_out, m_out)):
        band[kind] = jnp.zeros(band.shape[1:], band.dtype)
        for p in range(len(PAIRS)):
            chunk = pl.ds((kind * len(PAIRS) + p) * SPLIT, SPLIT)
            for place in range(owners * slots):
                at = targets[p, place]
                band[kind, at] += got[chunk, place // slots, place % slots].reshape(band.shape[2:])
        writes.append(pltpu.make_async_copy(band.at[kind, pl.ds(0, limit)], out, out_sems.at[kind]))
        writes[-1].start()
    for write in writes:
        write.wait()


def per_device(
    stiff_bb, stiff_bi, constraint_modes, interior_mass, fixed_modes, mass_bb, boundary_map
):
    owners = lax.axis_size("row")
    lanes = lax.axis_size("col")
    count, order, inner = stiff_bi.shape
    modes = fixed_modes.shape[2]
    width = order // 3
    part = width // lanes
    rows = part // SPLIT
    slots = (count * lanes + owners - 1) // owners
    f32, bf16 = jnp.float32, jnp.bfloat16
    hbm = pl.BlockSpec(memory_space=pltpu.HBM)
    vmem = pl.BlockSpec(memory_space=pltpu.VMEM)
    smem = pl.BlockSpec(memory_space=pltpu.SMEM)
    dma = pltpu.SemaphoreType.DMA
    got, targets, coupled = pl.pallas_call(
        functools.partial(reduce_and_send, owners, lanes, slots),
        out_shape=(
            pltpu.VMEM((CHUNKS, owners, slots, rows, width), f32),
            jax.ShapeDtypeStruct((len(PAIRS), owners * slots), jnp.int32),
            pltpu.VMEM((count, modes, order), f32),
        ),
        in_specs=[hbm] * 7,
        out_specs=(vmem, smem, vmem),
        scratch_shapes=[
            pltpu.VMEM((count, 3, width, order), bf16),
            pltpu.VMEM((count, order, inner), bf16),
            pltpu.VMEM((count, inner, order), bf16),
            pltpu.VMEM((count, inner, modes), bf16),
            pltpu.VMEM((count, 3, width, order), bf16),
            pltpu.VMEM((count, inner), f32),
            pltpu.VMEM((count, inner, order), bf16),
            pltpu.VMEM((CHUNKS, lanes, count, rows, width), f32),
            pltpu.VMEM((CHUNKS, lanes, count, rows, width), f32),
            pltpu.VMEM((lanes * count, rows, width), f32),
            pltpu.VMEM((CHUNKS, owners, slots, rows, width), f32),
            pltpu.VMEM((8, LANE), jnp.int32),
            pltpu.VMEM((lanes, 8, LANE), jnp.int32),
            pltpu.VMEM((owners, lanes, 8, LANE), jnp.int32),
            pltpu.SMEM((count, 3), jnp.int32),
            pltpu.SMEM((lanes, 8, LANE), jnp.int32),
            pltpu.SMEM((owners, lanes, 1, LANE), jnp.int32),
            dma((2, count)),
            dma,
            dma((CHUNKS,)),
            dma((2,)),
            dma((4,)),
            dma((8,)),
            dma((3,)),
        ],
        compiler_params=pltpu.CompilerParams(
            collective_id=0, has_side_effects=True, vmem_limit_bytes=VMEM_LIMIT
        ),
        name="reduce_and_send",
    )(*(
        pltpu.with_memory_space_constraint(x, pltpu.HBM)
        for x in (stiff_bb, stiff_bi, constraint_modes, interior_mass, fixed_modes, mass_bb, boundary_map)
    ))
    block = jax.ShapeDtypeStruct((BPO * BAND, part, width), f32)
    k_out, m_out, coupling = pl.pallas_call(
        functools.partial(assemble, owners, slots),
        out_shape=(block, block, jax.ShapeDtypeStruct(coupled.shape, f32)),
        in_specs=[smem, vmem, vmem],
        out_specs=(hbm, hbm, hbm),
        scratch_shapes=[
            pltpu.VMEM((KINDS, BPO * BAND + 1, part, width), f32),
            dma((KINDS + 1,)),
        ],
        compiler_params=pltpu.CompilerParams(vmem_limit_bytes=BAND_LIMIT),
        name="assemble",
    )(targets, got, coupled)
    shape = (BPO, BAND, part, width)
    return k_out.reshape(shape), m_out.reshape(shape), coupling


def solution(mesh):
    placed = (
        P(("row", "col"), None, None, None),
        P(("row", "col"), None, None),
        P(("row", "col"), None, None),
        P(("row", "col"), None),
        P(("row", "col"), None, None),
        P(("row", "col"), None, None, None),
        P(("row", "col"), None),
    )
    return jax.shard_map(
        per_device,
        mesh=mesh,
        in_specs=placed,
        out_specs=(
            P("row", None, "col", None),
            P("row", None, "col", None),
            P(("row", "col"), None, None),
        ),
        check_vma=False,
    )
```

time: 71.2 us -> 67.4 us (0.947)
  Pallas kernels: 70.3 us -> 66.8 us
    pallas_call x1, Pallas kernels: 65.7 us -> 63.8 us  [per_device(): pl.pallas_call(functools.partial(reduce_and_send, owners, lanes, slots),...]
    pallas_call x1, Pallas kernels: 4.62 us -> 3 us  [per_device(): pl.pallas_call(functools.partial(assemble, owners, slots), out_shape=(blo...]
where the time goes in v2:
time: 67.4 us
  Pallas kernels  66.8 us (99%)
    pallas_call x1, Pallas kernels, per_device(): pl.pallas_call(functools.partial(reduce_and_send, owners, lanes, slots),...  63.8 us
    pallas_call x1, Pallas kernels, per_device(): pl.pallas_call(functools.partial(assemble, owners, slots), out_shape=(blo...  3 us

profile of v2, /device:TPU:0, one launch (start us, length us, event | category | flops | bytes accessed | tf_op | source)
XLA Modules:
  0.0 67.4 jit_solution(1213508420488287416)
XLA Ops:
  0.6 63.8 %reduce_and_send.1 = (f32[12,8,2,32,128]{4,3,2,1,0:T(8,128)S(1)}, s32[6,16]{1,0:T(8,128)S(1)}, f32[3,256,384]{2,1,0:T(8,128)S(1)}) custom-call(bf16[3,3,128,384]{3,2,1,0:T(8,128)(2,1)} %kbb.1, bf16[3,384,3072]{2,1,0:T(8,128)(2,1)} %kbi.1, bf16[3,3072,384]{2,1,0:T(8,128)(2,1)} %psi.1, f32[3,3072]{1,0:T(4,128)} %mass.1, bf16[3,3072,256]{2,1,0:T(8,128)(2,1)} %modes.1, ...), custom_call_target="tpu_custom_call" | custom-call | tf_op jit(solution)/shard_map/reduce_and_send/pallas_call | solution.py:345
  64.4 3.0 %assemble.1 = (f32[96,32,128]{2,1,0:T(8,128)}, f32[96,32,128]{2,1,0:T(8,128)}, f32[3,256,384]{2,1,0:T(8,128)}) custom-call(s32[6,16]{1,0:T(8,128)S(1)} %get-tuple-element.9.targets, f32[12,8,2,32,128]{4,3,2,1,0:T(8,128)S(1)} %get-tuple-element.10.got, f32[3,256,384]{2,1,0:T(8,128)S(1)} %get-tuple-element.11.coupled), custom_call_target="tpu_custom_call" | custom-call | tf_op jit(solution)/shard_map/assemble/pallas_call | solution.py:389

commit v3 on v2

--- a/solution.py
+++ b/solution.py
@@ -16,10 +16,9 @@
 CHUNKS = KINDS * len(PAIRS) * SPLIT
 AHEAD = 2
 LEAD = 4
-PIECES = 4
 MESH = pl.DeviceIdType.MESH
-VMEM_LIMIT = 46 * 1024 * 1024
-BAND_LIMIT = 12 * 1024 * 1024
+VMEM_LIMIT = 55 * 1024 * 1024
+BAND_LIMIT = 1024 * 1024
 
 
 def at_col(z):
@@ -33,7 +32,8 @@
 def reduce_and_send(
     owners, lanes, slots,
     kbb, kbi, psi, mass, modes, mbb, table,
-    got, targets, coupled,
+    k_band, m_band, coupled,
+    got, totals, targets, links_v, links_s,
     kbb_v, kbi_v, psi_v, modes_v, mbb_v, mass_v, weighted,
     reduced, grouped, staging, outgoing, table_v, maps_v, all_v, table_s, maps_s, all_s,
     load_sems, z_send, z_recv, r_sems, map_sems, small, block_sems,
@@ -48,11 +48,10 @@
 
     def block_load(i):
         span = pl.ds(i * width, width)
-        return pltpu.make_async_copy(kbi.at[0, span], kbi_v.at[0, span], block_sems.at[i])
-
-    def piece_load(k):
-        span = pl.ds(k * (inner // PIECES), inner // PIECES)
-        return pltpu.make_async_copy(psi.at[0, span], psi_v.at[0, span], load_sems.at[1, 0])
+        return (
+            pltpu.make_async_copy(kbi.at[0, span], kbi_v.at[0, span], block_sems.at[0, i]),
+            pltpu.make_async_copy(psi.at[0, :, span], psi_v.at[0, :, span], block_sems.at[1, i]),
+        )
 
     def loads(s):
         return (
@@ -69,14 +68,11 @@
         pltpu.make_async_copy(modes, modes_v, small.at[4]),
     )
 
+    for copy in block_load(2):
+        copy.start()
+    first_kbb.start()
     table_load = pltpu.make_async_copy(table, table_s, small.at[5])
     table_load.start()
-    block_load(0).start()
-    for k in range(PIECES):
-        piece_load(k).start()
-    first_kbb.start()
-    for i in range(1, 3):
-        block_load(i).start()
 
     barrier = pltpu.get_barrier_semaphore()
     for i in range(1, lanes):
@@ -136,6 +132,9 @@
 
     half = CHUNKS // KINDS
     table_load.wait()
+    for i in (1, 0):
+        for copy in block_load(i):
+            copy.start()
     place = (lax.broadcasted_iota(jnp.int32, (8, LANE), 0), lax.broadcasted_iota(jnp.int32, (8, LANE), 1))
     tile = jnp.zeros((8, LANE), jnp.int32)
     for s in range(count):
@@ -144,11 +143,11 @@
     table_v[...] = tile
     maps_v[col] = tile
 
-    loads(0)[1].wait()
     first_kbb.wait()
-    for i in range(3):
-        block_load(i).wait()
-        if i == 0:
+    for i in reversed(range(3)):
+        for copy in block_load(i):
+            copy.wait()
+        if i == 1:
             for later in range(1, count):
                 for copy in loads(later):
                     copy.start()
@@ -156,7 +155,7 @@
             for copy in late_loads:
                 copy.start()
         stiff(0, i)
-        if i == 0:
+        if i == 2:
             pl.semaphore_wait(barrier, lanes - 1 + owners - 1)
             for k in range(1, lanes):
                 z_map(k).start()
@@ -264,11 +263,14 @@
         got[p, row] = outgoing[p, row]
         return carry
 
+    def arrival(p):
+        return jnp.where(p < half, 1, jnp.where(p < CHUNKS - SPLIT, 2, 3))
+
     def r_copy(p, i):
         to = lax.rem(row + i, owners)
         return pltpu.make_async_remote_copy(
             src_ref=outgoing.at[p, to], dst_ref=got.at[p, row],
-            send_sem=r_sems.at[0], recv_sem=r_sems.at[1],
+            send_sem=r_sems.at[0], recv_sem=r_sems.at[arrival(p)],
             device_id=at_row(to), device_id_type=MESH,
         )
 
@@ -277,6 +279,43 @@
     all_scalar = pltpu.make_async_copy(all_v.at[:, :, pl.ds(0, 1)], all_s, small.at[7])
     all_scalar.start()
     all_scalar.wait()
+
+    seats = owners * slots
+    entries = len(PAIRS) * seats
+    extent = entries + -entries % LANE
+    limit = BPO * BAND
+
+    def links():
+        goals = [targets[c // seats, c % seats] for c in range(entries)]
+        lane = lax.broadcasted_iota(jnp.int32, (8, extent), 1)
+        sub = lax.broadcasted_iota(jnp.int32, (8, extent), 0)
+        along = jnp.full((8, extent), -1, jnp.int32)
+        for c in range(entries):
+            along = jnp.where(lane == c, goals[c], along)
+        before = jnp.full((8, extent), -1, jnp.int32)
+        final = jnp.full((8, extent), -1, jnp.int32)
+        for base in range(0, entries, 8):
+            down = jnp.full((8, extent), -2, jnp.int32)
+            for r in range(8):
+                down = jnp.where(sub == r, goals[base + r], down)
+            entry = sub + base
+            before = jnp.where((down == along) & (entry < lane), entry, before)
+            final = jnp.where(down == lane, entry, final)
+        for kind, found in enumerate((before, final)):
+            best = found[0:1]
+            for r in range(1, 8):
+                best = jnp.maximum(best, found[r : r + 1])
+            links_v[kind : kind + 1] = jnp.where(best < 0, entries, best)
+        to_links = pltpu.make_async_copy(links_v, links_s, small.at[6])
+        to_links.start()
+        to_links.wait()
+
+    def chain(kind, p, carry):
+        for seat in range(seats):
+            c = p * seats + seat
+            piece = got[pl.ds((kind * len(PAIRS) + p) * SPLIT, SPLIT), seat // slots, seat % slots]
+            totals[kind, c] = piece.reshape(part, width) + totals[kind, links_s[0, c]]
+        return carry
 
     def aim(group, carry):
         picked = [[jnp.int32(-1)] * 3 for _ in range(slots)]
@@ -296,6 +335,8 @@
         return carry
 
     lax.fori_loop(0, owners, aim, 0)
+    links()
+
     def follow(first, last, send):
         lax.fori_loop(first, last, functools.partial(forward, send), 0)
 
@@ -304,24 +345,39 @@
     follow(half - AHEAD, CHUNKS - AHEAD, lambda p: send_chunk(p + AHEAD))
     follow(CHUNKS - AHEAD, CHUNKS, None)
 
+    def arrived(first, last, k):
+        drain(got.at[pl.ds(first, last - first), pl.ds(0, owners - 1)], r_sems.at[k])
+
+    def gather(kind, band, first, last):
+        def row_block(g, carry):
+            for d in range(first, last):
+                band[g * BAND + d] = totals[kind, links_s[1, g * BAND + d]]
+            return carry
+
+        lax.fori_loop(0, BPO, row_block, 0)
+
+    for kind in range(KINDS):
+        totals[kind, entries] = jnp.zeros((part, width), jnp.float32)
+    arrived(0, half, 1)
+    lax.fori_loop(0, len(PAIRS), functools.partial(chain, 0), 0)
+    gather(0, k_band, 0, BAND)
+    arrived(half, CHUNKS - SPLIT, 2)
+    lax.fori_loop(0, len(PAIRS) - 1, functools.partial(chain, 1), 0)
+    gather(1, m_band, 0, 2)
     drain(grouped.at[:, pl.ds(0, lanes - 1)], z_send)
-    for k in range(2):
-        drain(got.at[:, pl.ds(0, owners - 1)], r_sems.at[k])
-
-
-def assemble(owners, slots, targets, got, coupled, k_out, m_out, coupling, band, out_sems):
-    limit = BPO * BAND
-    writes = [pltpu.make_async_copy(coupled, coupling, out_sems.at[KINDS])]
-    writes[0].start()
-    for kind, out in enumerate((k_out, m_out)):
-        band[kind] = jnp.zeros(band.shape[1:], band.dtype)
-        for p in range(len(PAIRS)):
-            chunk = pl.ds((kind * len(PAIRS) + p) * SPLIT, SPLIT)
-            for place in range(owners * slots):
-                at = targets[p, place]
-                band[kind, at] += got[chunk, place // slots, place % slots].reshape(band.shape[2:])
-        writes.append(pltpu.make_async_copy(band.at[kind, pl.ds(0, limit)], out, out_sems.at[kind]))
-        writes[-1].start()
+    arrived(CHUNKS - SPLIT, CHUNKS, 3)
+    chain(1, len(PAIRS) - 1, 0)
+    gather(1, m_band, 2, BAND)
+    drain(got.at[:, pl.ds(0, owners - 1)], r_sems.at[0])
+
+
+def hand_out(k_band, m_band, coupled, k_out, m_out, coupling, sems):
+    writes = [
+        pltpu.make_async_copy(source, out, sems.at[i])
+        for i, (source, out) in enumerate(((k_band, k_out), (m_band, m_out), (coupled, coupling)))
+    ]
+    for write in writes:
+        write.start()
     for write in writes:
         write.wait()
 
@@ -340,18 +396,26 @@
     f32, bf16 = jnp.float32, jnp.bfloat16
     hbm = pl.BlockSpec(memory_space=pltpu.HBM)
     vmem = pl.BlockSpec(memory_space=pltpu.VMEM)
-    smem = pl.BlockSpec(memory_space=pltpu.SMEM)
     dma = pltpu.SemaphoreType.DMA
-    got, targets, coupled = pl.pallas_call(
+    seats = owners * slots
+    entries = len(PAIRS) * seats
+    extent = entries + -entries % LANE
+    band = pltpu.VMEM((BPO * BAND, part, width), f32)
+    bands = pl.pallas_call(
         functools.partial(reduce_and_send, owners, lanes, slots),
         out_shape=(
-            pltpu.VMEM((CHUNKS, owners, slots, rows, width), f32),
-            jax.ShapeDtypeStruct((len(PAIRS), owners * slots), jnp.int32),
+            band,
+            band,
             pltpu.VMEM((count, modes, order), f32),
         ),
         in_specs=[hbm] * 7,
-        out_specs=(vmem, smem, vmem),
+        out_specs=(vmem, vmem, vmem),
         scratch_shapes=[
+            pltpu.VMEM((CHUNKS, owners, slots, rows, width), f32),
+            pltpu.VMEM((KINDS, entries + 1, part, width), f32),
+            pltpu.SMEM((len(PAIRS), seats), jnp.int32),
+            pltpu.VMEM((KINDS, extent), jnp.int32),
+            pltpu.SMEM((KINDS, extent), jnp.int32),
             pltpu.VMEM((count, 3, width, order), bf16),
             pltpu.VMEM((count, order, inner), bf16),
             pltpu.VMEM((count, inner, order), bf16),
@@ -372,10 +436,10 @@
             dma((2, count)),
             dma,
             dma((CHUNKS,)),
-            dma((2,)),
+            dma((4,)),
             dma((4,)),
             dma((8,)),
-            dma((3,)),
+            dma((2, 3)),
         ],
         compiler_params=pltpu.CompilerParams(
             collective_id=0, has_side_effects=True, vmem_limit_bytes=VMEM_LIMIT
@@ -385,19 +449,16 @@
         pltpu.with_memory_space_constraint(x, pltpu.HBM)
         for x in (stiff_bb, stiff_bi, constraint_modes, interior_mass, fixed_modes, mass_bb, boundary_map)
     ))
-    block = jax.ShapeDtypeStruct((BPO * BAND, part, width), f32)
+    block = jax.ShapeDtypeStruct(band.shape, f32)
     k_out, m_out, coupling = pl.pallas_call(
-        functools.partial(assemble, owners, slots),
-        out_shape=(block, block, jax.ShapeDtypeStruct(coupled.shape, f32)),
-        in_specs=[smem, vmem, vmem],
+        hand_out,
+        out_shape=(block, block, jax.ShapeDtypeStruct((count, modes, order), f32)),
+        in_specs=[vmem] * 3,
         out_specs=(hbm, hbm, hbm),
-        scratch_shapes=[
-            pltpu.VMEM((KINDS, BPO * BAND + 1, part, width), f32),
-            dma((KINDS + 1,)),
-        ],
+        scratch_shapes=[dma((3,))],
         compiler_params=pltpu.CompilerParams(vmem_limit_bytes=BAND_LIMIT),
-        name="assemble",
-    )(targets, got, coupled)
+        name="hand_out",
+    )(*bands)
     shape = (BPO, BAND, part, width)
     return k_out.reshape(shape), m_out.reshape(shape), coupling
 

time: 67.4 us -> 66.4 us (0.985)
  Pallas kernels: 66.8 us -> 65.6 us
    pallas_call x1, Pallas kernels: 3 us -> 2.08 us  [per_device(): pl.pallas_call(hand_out, out_shape=(block, block, jax.ShapeDtypeStruct((c...]
where the time goes in v3:
time: 66.4 us; the launch traced here: 66.2 us
  Pallas kernels  65.6 us (99%)
    pallas_call x1, Pallas kernels, per_device(): pl.pallas_call(functools.partial(reduce_and_send, owners, lanes, slots),...  63.5 us
    pallas_call x1, Pallas kernels, per_device(): pl.pallas_call(hand_out, out_shape=(block, block, jax.ShapeDtypeStruct((c...  2.08 us

profile of v3, /device:TPU:0, one launch (start us, length us, event | category | flops | bytes accessed | tf_op | source)
XLA Modules:
  0.0 66.2 jit_solution(2685097536800453520)
XLA Ops:
  0.6 63.5 %reduce_and_send.1 = (f32[96,32,128]{2,1,0:T(8,128)S(1)}, f32[96,32,128]{2,1,0:T(8,128)S(1)}, f32[3,256,384]{2,1,0:T(8,128)S(1)}) custom-call(bf16[3,3,128,384]{3,2,1,0:T(8,128)(2,1)} %kbb.1, bf16[3,384,3072]{2,1,0:T(8,128)(2,1)} %kbi.1, bf16[3,3072,384]{2,1,0:T(8,128)(2,1)} %psi.1, f32[3,3072]{1,0:T(4,128)} %mass.1, bf16[3,3072,256]{2,1,0:T(8,128)(2,1)} %modes.1, ...), custom_call_target="tpu_custom_call" | custom-call | tf_op jit(solution)/shard_map/reduce_and_send/pallas_call | solution.py:404
  64.1 2.1 %hand_out.1 = (f32[96,32,128]{2,1,0:T(8,128)}, f32[96,32,128]{2,1,0:T(8,128)}, f32[3,256,384]{2,1,0:T(8,128)}) custom-call(f32[96,32,128]{2,1,0:T(8,128)S(1)} %get-tuple-element.9.k_band, f32[96,32,128]{2,1,0:T(8,128)S(1)} %get-tuple-element.10.m_band, f32[3,256,384]{2,1,0:T(8,128)S(1)} %get-tuple-element.11.coupled), custom_call_target="tpu_custom_call" | custom-call | tf_op jit(solution)/shard_map/hand_out/pallas_call | solution.py:453

commit v4 on v3

--- a/solution.py
+++ b/solution.py
@@ -16,6 +16,7 @@
 CHUNKS = KINDS * len(PAIRS) * SPLIT
 AHEAD = 2
 LEAD = 4
+TURN = 3
 MESH = pl.DeviceIdType.MESH
 VMEM_LIMIT = 55 * 1024 * 1024
 BAND_LIMIT = 1024 * 1024
@@ -175,16 +176,19 @@
 
     lax.fori_loop(1, count, stiffs, 0)
 
-    def send_rest(p):
-        for i in range(1, lanes):
-            z_copy_part(p, 1, count - 1, i).start()
-
-    def send_chunk(p):
-        for i in range(1, lanes):
-            z_copy(p, i).start()
+    def send(p):
+        @pl.when(p < half)
+        def _():
+            for k in range(1, lanes):
+                z_copy_part(p, 1, count - 1, k).start()
+
+        @pl.when(p >= half)
+        def _():
+            for k in range(1, lanes):
+                z_copy(p, k).start()
 
     for p in range(LEAD):
-        send_rest(p)
+        send(p)
 
     def masses(s, carry):
         pick = lax.broadcasted_iota(jnp.int32, (count, inner), 0) == s
@@ -246,10 +250,10 @@
             member = jnp.where(places[m] == slot, m, member)
         chosen.append(member)
 
-    def forward(send, p, carry):
+    def forward(ahead, p, carry):
         drain(grouped.at[p, pl.ds(0, lanes - 1)], z_recv.at[p])
-        if send is not None:
-            send(p)
+        if ahead is not None:
+            send(p + ahead)
 
         staging[...] = grouped[p].reshape(members, rows, width)
         for slot, member in enumerate(chosen):
@@ -337,13 +341,17 @@
     lax.fori_loop(0, owners, aim, 0)
     links()
 
-    def follow(first, last, send):
-        lax.fori_loop(first, last, functools.partial(forward, send), 0)
-
-    follow(0, half - LEAD, lambda p: send_rest(p + LEAD))
-    follow(half - LEAD, half - AHEAD, None)
-    follow(half - AHEAD, CHUNKS - AHEAD, lambda p: send_chunk(p + AHEAD))
-    follow(CHUNKS - AHEAD, CHUNKS, None)
+    issued = LEAD
+    steps = []
+    for p in range(CHUNKS):
+        wanted = min(p + 1 + (LEAD if p < half - LEAD else TURN if p < half - 1 else AHEAD), CHUNKS)
+        steps.append(issued - p if wanted > issued else None)
+        issued = max(issued, wanted if wanted <= issued + 1 else issued + 1)
+    first = 0
+    for p in range(1, CHUNKS + 1):
+        if p == CHUNKS or steps[p] != steps[first]:
+            lax.fori_loop(first, p, functools.partial(forward, steps[first]), 0)
+            first = p
 
     def arrived(first, last, k):
         drain(got.at[pl.ds(first, last - first), pl.ds(0, owners - 1)], r_sems.at[k])

time: 66.4 us -> 65.4 us (0.985)
  Pallas kernels: 65.6 us -> 64.6 us
    pallas_call x1, Pallas kernels: 63.5 us -> 62.5 us  [per_device(): pl.pallas_call(functools.partial(reduce_and_send, owners, lanes, slots),...]
where the time goes in v4:
time: 65.4 us; the launch traced here: 65.2 us
  Pallas kernels  64.6 us (99%)
    pallas_call x1, Pallas kernels, per_device(): pl.pallas_call(functools.partial(reduce_and_send, owners, lanes, slots),...  62.5 us
    pallas_call x1, Pallas kernels, per_device(): pl.pallas_call(hand_out, out_shape=(block, block, jax.ShapeDtypeStruct((c...  2.08 us

profile of v4, /device:TPU:0, one launch (start us, length us, event | category | flops | bytes accessed | tf_op | source)
XLA Modules:
  0.0 65.2 jit_solution(13691038872557316903)
XLA Ops:
  0.6 62.5 %reduce_and_send.1 = (f32[96,32,128]{2,1,0:T(8,128)S(1)}, f32[96,32,128]{2,1,0:T(8,128)S(1)}, f32[3,256,384]{2,1,0:T(8,128)S(1)}) custom-call(bf16[3,3,128,384]{3,2,1,0:T(8,128)(2,1)} %kbb.1, bf16[3,384,3072]{2,1,0:T(8,128)(2,1)} %kbi.1, bf16[3,3072,384]{2,1,0:T(8,128)(2,1)} %psi.1, f32[3,3072]{1,0:T(4,128)} %mass.1, bf16[3,3072,256]{2,1,0:T(8,128)(2,1)} %modes.1, ...), custom_call_target="tpu_custom_call" | custom-call | tf_op jit(solution)/shard_map/reduce_and_send/pallas_call | solution.py:412
  63.1 2.1 %hand_out.1 = (f32[96,32,128]{2,1,0:T(8,128)}, f32[96,32,128]{2,1,0:T(8,128)}, f32[3,256,384]{2,1,0:T(8,128)}) custom-call(f32[96,32,128]{2,1,0:T(8,128)S(1)} %get-tuple-element.9.k_band, f32[96,32,128]{2,1,0:T(8,128)S(1)} %get-tuple-element.10.m_band, f32[3,256,384]{2,1,0:T(8,128)S(1)} %get-tuple-element.11.coupled), custom_call_target="tpu_custom_call" | custom-call | tf_op jit(solution)/shard_map/hand_out/pallas_call | solution.py:461

commit v5 on v4

--- a/solution.py
+++ b/solution.py
@@ -12,11 +12,10 @@
 
 PAIRS = ((0, 0), (0, 1), (1, 1), (1, 2), (2, 2), (0, 2))
 KINDS = 2
-SPLIT = 1
-CHUNKS = KINDS * len(PAIRS) * SPLIT
-AHEAD = 2
+CHUNKS = KINDS * len(PAIRS)
+LAST = CHUNKS - 1
+STEPS = (4, 5, None, 6, None, 7, 8, 9, 10, 11, None, None)
 LEAD = 4
-TURN = 3
 MESH = pl.DeviceIdType.MESH
 VMEM_LIMIT = 55 * 1024 * 1024
 BAND_LIMIT = 1024 * 1024
@@ -42,7 +41,6 @@
     count, order, inner = kbi.shape
     width = order // 3
     part = width // lanes
-    rows = part // SPLIT
     members = count * lanes
     row = lax.axis_index("row")
     col = lax.axis_index("col")
@@ -56,8 +54,8 @@
 
     def loads(s):
         return (
-            pltpu.make_async_copy(kbi.at[s], kbi_v.at[s], load_sems.at[0, s]),
-            pltpu.make_async_copy(psi.at[s], psi_v.at[s], load_sems.at[1, s]),
+            pltpu.make_async_copy(kbi.at[s], kbi_v.at[s], load_sems.at[0, s - 1]),
+            pltpu.make_async_copy(psi.at[s], psi_v.at[s], load_sems.at[1, s - 1]),
         )
 
     first_kbb = pltpu.make_async_copy(kbb.at[0], kbb_v.at[0], small.at[0])
@@ -87,9 +85,8 @@
 
     def put(kind, s, i, strip):
         for j in range(i, 3):
-            block = strip[:, (j - i) * width : (j - i + 1) * width].reshape(lanes, SPLIT, rows, width)
-            for h in range(SPLIT):
-                reduced[(kind * len(PAIRS) + PAIRS.index((i, j))) * SPLIT + h, :, s] = block[:, h]
+            block = strip[:, (j - i) * width : (j - i + 1) * width]
+            reduced[kind * len(PAIRS) + PAIRS.index((i, j)), :, s] = block.reshape(lanes, part, width)
 
     def stiff(s, i):
         strip = jnp.dot(
@@ -161,9 +158,8 @@
             for k in range(1, lanes):
                 z_map(k).start()
         for j in range(i, 3):
-            for h in range(SPLIT):
-                for k in range(1, lanes):
-                    z_copy_part(PAIRS.index((i, j)) * SPLIT + h, 0, 1, k).start()
+            for k in range(1, lanes):
+                z_copy_part(PAIRS.index((i, j)), 0, 1, k).start()
 
     other_kbb.wait()
 
@@ -216,7 +212,7 @@
 
     for k in range(2):
         drain(maps_v.at[pl.ds(0, lanes - 1)], map_sems.at[k])
-    to_scalar = pltpu.make_async_copy(maps_v, maps_s, small.at[6])
+    to_scalar = pltpu.make_async_copy(maps_v, maps_s, small.at[5])
     to_scalar.start()
     lax.fori_loop(1, owners, lambda i, c: (r_map(i).start(), c)[1], 0)
     all_v[row] = maps_v[...]
@@ -255,7 +251,7 @@
         if ahead is not None:
             send(p + ahead)
 
-        staging[...] = grouped[p].reshape(members, rows, width)
+        staging[...] = grouped[p].reshape(members, part, width)
         for slot, member in enumerate(chosen):
             outgoing[p, slot // slots, slot % slots] = staging[member]
 
@@ -268,7 +264,7 @@
         return carry
 
     def arrival(p):
-        return jnp.where(p < half, 1, jnp.where(p < CHUNKS - SPLIT, 2, 3))
+        return jnp.where(p < half, 1, jnp.where(p < LAST, 2, 3))
 
     def r_copy(p, i):
         to = lax.rem(row + i, owners)
@@ -280,7 +276,7 @@
 
     for k in range(2, 4):
         drain(all_v.at[pl.ds(0, owners - 1)], map_sems.at[k])
-    all_scalar = pltpu.make_async_copy(all_v.at[:, :, pl.ds(0, 1)], all_s, small.at[7])
+    all_scalar = pltpu.make_async_copy(all_v.at[:, :, pl.ds(0, 1)], all_s, small.at[5])
     all_scalar.start()
     all_scalar.wait()
 
@@ -310,15 +306,15 @@
             for r in range(1, 8):
                 best = jnp.maximum(best, found[r : r + 1])
             links_v[kind : kind + 1] = jnp.where(best < 0, entries, best)
-        to_links = pltpu.make_async_copy(links_v, links_s, small.at[6])
+        to_links = pltpu.make_async_copy(links_v, links_s, small.at[5])
         to_links.start()
         to_links.wait()
 
     def chain(kind, p, carry):
         for seat in range(seats):
             c = p * seats + seat
-            piece = got[pl.ds((kind * len(PAIRS) + p) * SPLIT, SPLIT), seat // slots, seat % slots]
-            totals[kind, c] = piece.reshape(part, width) + totals[kind, links_s[0, c]]
+            piece = got[kind * len(PAIRS) + p, seat // slots, seat % slots]
+            totals[kind, c] = piece + totals[kind, links_s[0, c]]
         return carry
 
     def aim(group, carry):
@@ -341,12 +337,7 @@
     lax.fori_loop(0, owners, aim, 0)
     links()
 
-    issued = LEAD
-    steps = []
-    for p in range(CHUNKS):
-        wanted = min(p + 1 + (LEAD if p < half - LEAD else TURN if p < half - 1 else AHEAD), CHUNKS)
-        steps.append(issued - p if wanted > issued else None)
-        issued = max(issued, wanted if wanted <= issued + 1 else issued + 1)
+    steps = [None if c is None else c - p for p, c in enumerate(STEPS)]
     first = 0
     for p in range(1, CHUNKS + 1):
         if p == CHUNKS or steps[p] != steps[first]:
@@ -369,11 +360,11 @@
     arrived(0, half, 1)
     lax.fori_loop(0, len(PAIRS), functools.partial(chain, 0), 0)
     gather(0, k_band, 0, BAND)
-    arrived(half, CHUNKS - SPLIT, 2)
+    arrived(half, LAST, 2)
     lax.fori_loop(0, len(PAIRS) - 1, functools.partial(chain, 1), 0)
     gather(1, m_band, 0, 2)
     drain(grouped.at[:, pl.ds(0, lanes - 1)], z_send)
-    arrived(CHUNKS - SPLIT, CHUNKS, 3)
+    arrived(LAST, CHUNKS, 3)
     chain(1, len(PAIRS) - 1, 0)
     gather(1, m_band, 2, BAND)
     drain(got.at[:, pl.ds(0, owners - 1)], r_sems.at[0])
@@ -399,7 +390,6 @@
     modes = fixed_modes.shape[2]
     width = order // 3
     part = width // lanes
-    rows = part // SPLIT
     slots = (count * lanes + owners - 1) // owners
     f32, bf16 = jnp.float32, jnp.bfloat16
     hbm = pl.BlockSpec(memory_space=pltpu.HBM)
@@ -419,7 +409,7 @@
         in_specs=[hbm] * 7,
         out_specs=(vmem, vmem, vmem),
         scratch_shapes=[
-            pltpu.VMEM((CHUNKS, owners, slots, rows, width), f32),
+            pltpu.VMEM((CHUNKS, owners, slots, part, width), f32),
             pltpu.VMEM((KINDS, entries + 1, part, width), f32),
             pltpu.SMEM((len(PAIRS), seats), jnp.int32),
             pltpu.VMEM((KINDS, extent), jnp.int32),
@@ -431,22 +421,22 @@
             pltpu.VMEM((count, 3, width, order), bf16),
             pltpu.VMEM((count, inner), f32),
             pltpu.VMEM((count, inner, order), bf16),
-            pltpu.VMEM((CHUNKS, lanes, count, rows, width), f32),
-            pltpu.VMEM((CHUNKS, lanes, count, rows, width), f32),
-            pltpu.VMEM((lanes * count, rows, width), f32),
-            pltpu.VMEM((CHUNKS, owners, slots, rows, width), f32),
+            pltpu.VMEM((CHUNKS, lanes, count, part, width), f32),
+            pltpu.VMEM((CHUNKS, lanes, count, part, width), f32),
+            pltpu.VMEM((lanes * count, part, width), f32),
+            pltpu.VMEM((CHUNKS, owners, slots, part, width), f32),
             pltpu.VMEM((8, LANE), jnp.int32),
             pltpu.VMEM((lanes, 8, LANE), jnp.int32),
             pltpu.VMEM((owners, lanes, 8, LANE), jnp.int32),
             pltpu.SMEM((count, 3), jnp.int32),
             pltpu.SMEM((lanes, 8, LANE), jnp.int32),
             pltpu.SMEM((owners, lanes, 1, LANE), jnp.int32),
-            dma((2, count)),
+            dma((2, count - 1)),
             dma,
             dma((CHUNKS,)),
             dma((4,)),
             dma((4,)),
-            dma((8,)),
+            dma((6,)),
             dma((2, 3)),
         ],
         compiler_params=pltpu.CompilerParams(

time: 65.4 us -> 65.1 us (level)
  no operation moved by 1% of the time
where the time goes in v5:
time: 65.1 us; the launch traced here: 64.9 us
  Pallas kernels  64.3 us (99%)
    pallas_call x1, Pallas kernels, per_device(): pl.pallas_call(functools.partial(reduce_and_send, owners, lanes, slots),...  62.2 us
    pallas_call x1, Pallas kernels, per_device(): pl.pallas_call(hand_out, out_shape=(block, block, jax.ShapeDtypeStruct((c...  2.08 us

profile of v5, /device:TPU:0, one launch (start us, length us, event | category | flops | bytes accessed | tf_op | source)
XLA Modules:
  0.0 64.9 jit_solution(7629298440979998279)
XLA Ops:
  0.6 62.2 %reduce_and_send.1 = (f32[96,32,128]{2,1,0:T(8,128)S(1)}, f32[96,32,128]{2,1,0:T(8,128)S(1)}, f32[3,256,384]{2,1,0:T(8,128)S(1)}) custom-call(bf16[3,3,128,384]{3,2,1,0:T(8,128)(2,1)} %kbb.1, bf16[3,384,3072]{2,1,0:T(8,128)(2,1)} %kbi.1, bf16[3,3072,384]{2,1,0:T(8,128)(2,1)} %psi.1, f32[3,3072]{1,0:T(4,128)} %mass.1, bf16[3,3072,256]{2,1,0:T(8,128)(2,1)} %modes.1, ...), custom_call_target="tpu_custom_call" | custom-call | tf_op jit(solution)/shard_map/reduce_and_send/pallas_call | solution.py:402
  62.8 2.1 %hand_out.1 = (f32[96,32,128]{2,1,0:T(8,128)}, f32[96,32,128]{2,1,0:T(8,128)}, f32[3,256,384]{2,1,0:T(8,128)}) custom-call(f32[96,32,128]{2,1,0:T(8,128)S(1)} %get-tuple-element.9.k_band, f32[96,32,128]{2,1,0:T(8,128)S(1)} %get-tuple-element.10.m_band, f32[3,256,384]{2,1,0:T(8,128)S(1)} %get-tuple-element.11.coupled), custom_call_target="tpu_custom_call" | custom-call | tf_op jit(solution)/shard_map/hand_out/pallas_call | solution.py:451

commit v6 on v5

--- a/solution.py
+++ b/solution.py
@@ -120,6 +120,17 @@
             send_sem=z_send, recv_sem=z_recv.at[p],
             device_id=at_col(to), device_id_type=MESH,
         )
+
+    def mirrored(i):
+        to, bit = 0, 1
+        while bit < owners:
+            to = to + lax.rem(row // bit + i // bit, 2) * bit
+            bit *= 2
+        return to
+
+    far_first = sorted(range(1, owners), key=lambda i: (-bin(i // 2).count("1"), -(i // 2), i))
+    paired = owners & (owners - 1) == 0
+    partners = [mirrored(i) if paired else lax.rem(row + i, owners) for i in far_first]
 
     def r_map(i):
         return pltpu.make_async_remote_copy(
@@ -255,19 +266,15 @@
         for slot, member in enumerate(chosen):
             outgoing[p, slot // slots, slot % slots] = staging[member]
 
-        def ship(i, inner_carry):
-            r_copy(p, i).start()
-            return inner_carry
-
-        lax.fori_loop(1, owners, ship, 0)
+        for to in partners:
+            r_copy(p, to).start()
         got[p, row] = outgoing[p, row]
         return carry
 
     def arrival(p):
         return jnp.where(p < half, 1, jnp.where(p < LAST, 2, 3))
 
-    def r_copy(p, i):
-        to = lax.rem(row + i, owners)
+    def r_copy(p, to):
         return pltpu.make_async_remote_copy(
             src_ref=outgoing.at[p, to], dst_ref=got.at[p, row],
             send_sem=r_sems.at[0], recv_sem=r_sems.at[arrival(p)],

time: 65.1 us -> 65.1 us (level)
  no operation moved by 1% of the time
where the time goes in v6:
time: 65.1 us; the launch traced here: 65 us
  Pallas kernels  64.3 us (99%)
    pallas_call x1, Pallas kernels, per_device(): pl.pallas_call(functools.partial(reduce_and_send, owners, lanes, slots),...  62.2 us
    pallas_call x1, Pallas kernels, per_device(): pl.pallas_call(hand_out, out_shape=(block, block, jax.ShapeDtypeStruct((c...  2.08 us

profile of v6, /device:TPU:0, one launch (start us, length us, event | category | flops | bytes accessed | tf_op | source)
XLA Modules:
  0.0 65.0 jit_solution(9733934057202317724)
XLA Ops:
  0.6 62.2 %reduce_and_send.1 = (f32[96,32,128]{2,1,0:T(8,128)S(1)}, f32[96,32,128]{2,1,0:T(8,128)S(1)}, f32[3,256,384]{2,1,0:T(8,128)S(1)}) custom-call(bf16[3,3,128,384]{3,2,1,0:T(8,128)(2,1)} %kbb.1, bf16[3,384,3072]{2,1,0:T(8,128)(2,1)} %kbi.1, bf16[3,3072,384]{2,1,0:T(8,128)(2,1)} %psi.1, f32[3,3072]{1,0:T(4,128)} %mass.1, bf16[3,3072,256]{2,1,0:T(8,128)(2,1)} %modes.1, ...), custom_call_target="tpu_custom_call" | custom-call | tf_op jit(solution)/shard_map/reduce_and_send/pallas_call | solution.py:409
  62.9 2.1 %hand_out.1 = (f32[96,32,128]{2,1,0:T(8,128)}, f32[96,32,128]{2,1,0:T(8,128)}, f32[3,256,384]{2,1,0:T(8,128)}) custom-call(f32[96,32,128]{2,1,0:T(8,128)S(1)} %get-tuple-element.9.k_band, f32[96,32,128]{2,1,0:T(8,128)S(1)} %get-tuple-element.10.m_band, f32[3,256,384]{2,1,0:T(8,128)S(1)} %get-tuple-element.11.coupled), custom_call_target="tpu_custom_call" | custom-call | tf_op jit(solution)/shard_map/hand_out/pallas_call | solution.py:458
